TPU v7x, 32 devices: a whole 2x2x4 slice. The times are simulated.
32 devices in a mesh: graph: 8 (over y, x, core), rep: 4 (over z).
Axes of the slice: x: 2, y: 2, z: 4, core: 2. Of those that a mesh axis runs over, the one named last changes fastest.
Arguments:
- nodes: bfloat16 [4, 64, 32, 256], P('rep', 'graph'), may hold values from -20 to 20, as said below
- cotangent: bfloat16 [4, 64, 32, 256], P('rep', 'graph'), may hold values from -6 to 6
- live: int32 [4, 64], P('rep', 'graph'), may hold values from 2 to 32, as said below
- partner_first: int32 [4, 64], P('rep', 'graph'), may hold values from 0 to 63, as said below
- partner_size: int32 [4, 64], P('rep', 'graph'), may hold values from 1 to 2
- edge_src: int32 [4, 2048], P('rep', 'graph'), may hold values from 0 to 255, as said below
- edge_dst: int32 [4, 2048], P('rep', 'graph'), may hold values from 0 to 255, as said below
- w_edge1: bfloat16 [512, 512], replicated, may hold values from -0.25 to 0.25
- b_edge: float32 [512], replicated, may hold values from -3 to 3
- w_edge2: bfloat16 [512, 256], replicated, may hold values from -0.25 to 0.25
- w_node1: bfloat16 [768, 512], replicated, may hold values from -0.21875 to 0.21875
- b_node: float32 [512], replicated, may hold values from -3 to 3
- w_node2: bfloat16 [512, 256], replicated, may hold values from -0.25 to 0.25
Outputs:
- updated: bfloat16 [4, 64, 32, 256], P('rep', 'graph')
- d_nodes: bfloat16 [4, 64, 32, 256], P('rep', 'graph')
- g_edge1: float32 [512, 512], P('rep')
- g_bedge: float32 [512], P('rep')
- g_edge2: float32 [512, 256], P('rep')
- g_node1: float32 [768, 512], P('rep')
- g_bnode: float32 [512], P('rep')
- g_node2: float32 [512, 256], P('rep')
Inputs may be any that keep to these rules, and one draw needn't show every extreme that they name: A graph is one or two consecutive granules of one device, and every granule of a graph but its last is full; rows beyond live are padding. `partner_first`: index within the replica of the first granule of the partner graph, the same for all granules of a graph; pairing is mutual. Graphs in the lower half of a device's 8 granules pair with graphs in the upper half of some device's granules; the upper-half graphs of one device have partners on distinct devices. Within a replica every half of every device holds the same number of two-granule graphs. `edge_src`: row index within the device (granule times 32 plus row); both ends of an edge are live rows of the same graph. `edge_dst`: as edge_src. `nodes`: padding rows are zero.
All inputs are finite; a program needn't handle non-finite values.
Results may differ from a plain program's by a relative error of at most 0.023.
Values may be sent and summed in bfloat16 or wider, within the bound.
A program may use at most 128 MiB of HBM per device.

v0:
```python
import jax
import jax.numpy as jnp
from jax import lax
from jax.sharding import PartitionSpec as P

GMAX = 2


def silu_slope(values):
    sigmoid_value = jax.nn.sigmoid(values)
    return sigmoid_value * (1.0 + values * (1.0 - sigmoid_value))


def attend(queries, key_rows, key_mask):
    scale_factor = queries.shape[-1] ** (-0.5)
    scores = (
        jnp.einsum("gqh,gkh->gqk", queries, key_rows, preferred_element_type=jnp.float32)
        * scale_factor
    )
    scores = jnp.where(key_mask[:, None, :], scores, -jnp.inf)
    highest = jnp.max(scores, axis=-1, keepdims=True)
    powers = jnp.exp(scores - highest)
    softmax_out = powers / jnp.sum(powers, axis=-1, keepdims=True)
    softmax_low = softmax_out.astype(jnp.bfloat16)
    context = jnp.einsum("gqk,gkh->gqh", softmax_low, key_rows, preferred_element_type=jnp.float32)
    moved_rows = (queries.astype(jnp.float32) - context).astype(jnp.bfloat16)
    return (moved_rows, softmax_out, softmax_low)


def attend_back(queries, key_rows, softmax_out, softmax_low, grad_moved):
    scale_factor = queries.shape[-1] ** (-0.5)
    negated = -grad_moved
    grad_probs = jnp.einsum("gqh,gkh->gqk", negated, key_rows, preferred_element_type=jnp.float32)
    grad_keys = jnp.einsum("gqk,gqh->gkh", softmax_low, negated, preferred_element_type=jnp.float32)
    inner_sum = jnp.sum(softmax_out * grad_probs, axis=-1, keepdims=True)
    grad_scores = (softmax_out * (grad_probs - inner_sum) * scale_factor).astype(jnp.bfloat16)
    grad_queries = jnp.einsum(
        "gqk,gkh->gqh", grad_scores, key_rows, preferred_element_type=jnp.float32
    ) + grad_moved.astype(jnp.float32)
    grad_keys = grad_keys + jnp.einsum(
        "gqk,gqh->gkh", grad_scores, queries, preferred_element_type=jnp.float32
    )
    return (grad_queries, grad_keys)


def message_forward(node_rows, w_edge1, b_edge, w_edge2, sources, targets):
    state_width = node_rows.shape[1]
    pre_target = (
        jnp.dot(node_rows, w_edge1[:state_width], preferred_element_type=jnp.float32) + b_edge
    ).astype(jnp.bfloat16)
    pre_source = jnp.dot(
        node_rows, w_edge1[state_width:], preferred_element_type=jnp.float32
    ).astype(jnp.bfloat16)
    summed = pre_target[targets].astype(jnp.float32) + pre_source[sources].astype(jnp.float32)
    gathered = jax.ops.segment_sum(
        jax.nn.silu(summed), targets, num_segments=node_rows.shape[0]
    ).astype(jnp.bfloat16)
    message = jnp.dot(gathered, w_edge2, preferred_element_type=jnp.float32).astype(jnp.bfloat16)
    return (message, gathered, summed)


def message_backward(node_rows, w_edge1, w_edge2, sources, targets, gathered, summed, grad_message):
    state_width = node_rows.shape[1]
    grad_w2 = jnp.einsum("rf,rh->fh", gathered, grad_message, preferred_element_type=jnp.float32)
    grad_gathered = jnp.einsum(
        "rh,fh->rf", grad_message, w_edge2, preferred_element_type=jnp.float32
    ).astype(jnp.bfloat16)
    edge_grad = grad_gathered[targets].astype(jnp.float32) * silu_slope(summed)
    grad_target = jax.ops.segment_sum(edge_grad, targets, num_segments=node_rows.shape[0]).astype(
        jnp.bfloat16
    )
    grad_source = jax.ops.segment_sum(edge_grad, sources, num_segments=node_rows.shape[0]).astype(
        jnp.bfloat16
    )
    grad_w1 = jnp.concatenate(
        [
            jnp.einsum("rh,rf->hf", node_rows, grad_target, preferred_element_type=jnp.float32),
            jnp.einsum("rh,rf->hf", node_rows, grad_source, preferred_element_type=jnp.float32),
        ],
        axis=0,
    )
    grad_bias = jnp.sum(grad_target.astype(jnp.float32), axis=0)
    grad_rows = jnp.einsum(
        "rf,hf->rh", grad_target, w_edge1[:state_width], preferred_element_type=jnp.float32
    ) + jnp.einsum(
        "rf,hf->rh", grad_source, w_edge1[state_width:], preferred_element_type=jnp.float32
    )
    return (grad_rows, grad_w1, grad_bias, grad_w2)


def update_forward(node_rows, message, moved_flat, w_node1, b_node, w_node2, row_mask):
    state_width = node_rows.shape[1]
    hidden_pre = (
        jnp.dot(node_rows, w_node1[:state_width], preferred_element_type=jnp.float32)
        + jnp.dot(
            message, w_node1[state_width : 2 * state_width], preferred_element_type=jnp.float32
        )
        + jnp.dot(moved_flat, w_node1[2 * state_width :], preferred_element_type=jnp.float32)
        + b_node
    )
    active = jax.nn.silu(hidden_pre).astype(jnp.bfloat16)
    updated = jnp.where(
        row_mask,
        node_rows.astype(jnp.float32)
        + jnp.dot(active, w_node2, preferred_element_type=jnp.float32),
        0.0,
    ).astype(jnp.bfloat16)
    return (updated, hidden_pre, active)


def update_backward(node_rows, message, moved_flat, w_node1, w_node2, hidden_pre, active, grad_out):
    state_width = node_rows.shape[1]
    grad_w2 = jnp.einsum("rf,rh->fh", active, grad_out, preferred_element_type=jnp.float32)
    grad_hidden = (
        jnp.einsum("rh,fh->rf", grad_out, w_node2, preferred_element_type=jnp.float32)
        * silu_slope(hidden_pre)
    ).astype(jnp.bfloat16)
    grad_w1 = jnp.concatenate(
        [
            jnp.einsum("rh,rf->hf", node_rows, grad_hidden, preferred_element_type=jnp.float32),
            jnp.einsum("rh,rf->hf", message, grad_hidden, preferred_element_type=jnp.float32),
            jnp.einsum("rh,rf->hf", moved_flat, grad_hidden, preferred_element_type=jnp.float32),
        ],
        axis=0,
    )
    grad_bias = jnp.sum(grad_hidden.astype(jnp.float32), axis=0)
    grad_rows = grad_out.astype(jnp.float32) + jnp.einsum(
        "rf,hf->rh", grad_hidden, w_node1[:state_width], preferred_element_type=jnp.float32
    )
    grad_message = jnp.einsum(
        "rf,hf->rh",
        grad_hidden,
        w_node1[state_width : 2 * state_width],
        preferred_element_type=jnp.float32,
    ).astype(jnp.bfloat16)
    grad_moved = jnp.einsum(
        "rf,hf->rh", grad_hidden, w_node1[2 * state_width :], preferred_element_type=jnp.float32
    ).astype(jnp.bfloat16)
    return (grad_rows, grad_message, grad_moved, grad_w1, grad_bias, grad_w2)


def on_device(
    nodes,
    cotangent,
    live,
    partner_first,
    partner_size,
    edge_src,
    edge_dst,
    w_edge1,
    b_edge,
    w_edge2,
    w_node1,
    b_node,
    w_node2,
):
    local_nodes = nodes[0]
    granules, block_rows, state_width = local_nodes.shape
    half_count = granules // 2
    peer_count = lax.axis_size("graph")
    live_counts = live[0]
    partners = partner_first[0]
    partner_device = partners // granules
    same_before = jnp.concatenate([jnp.zeros((1,), jnp.bool_), partners[1:] == partners[:-1]])
    place_index = same_before.astype(jnp.int32)
    positions = jnp.arange(block_rows, dtype=jnp.int32)
    spans = jnp.arange(GMAX, dtype=jnp.int32)
    row_mask = (positions[None, :] < live_counts[:, None]).reshape(-1, 1)
    node_rows = local_nodes.reshape(-1, state_width)
    sources = edge_src[0]
    targets = edge_dst[0]
    slot_count = peer_count * 2 * GMAX
    send_offset = jnp.where(jnp.arange(granules, dtype=jnp.int32) < half_count, GMAX, 0)
    send_slot = partner_device * (2 * GMAX) + send_offset + place_index
    outgoing = (
        jnp.zeros((slot_count, block_rows, state_width), jnp.bfloat16)
        .at[send_slot]
        .set(local_nodes)
    )
    lives_out = jnp.zeros((slot_count,), jnp.int32).at[send_slot].set(live_counts)
    arrived, arrived_lives = (
        lax.all_to_all(outgoing, "graph", split_axis=0, concat_axis=0, tiled=True),
        lax.all_to_all(lives_out, "graph", split_axis=0, concat_axis=0, tiled=True),
    )
    message, gathered, summed = message_forward(
        node_rows, w_edge1, b_edge, w_edge2, sources, targets
    )
    read_slot = (
        partner_device[:, None] * (2 * GMAX) + (GMAX - send_offset)[:, None] + spans[None, :]
    )
    keys_all = arrived[read_slot].reshape(granules, GMAX * block_rows, state_width)
    mask_all = (positions[None, None, :] < arrived_lives[read_slot][:, :, None]).reshape(
        granules, GMAX * block_rows
    )
    moved_rows, probs_all, low_all = attend(local_nodes, keys_all, mask_all)
    moved_flat = moved_rows.reshape(-1, state_width)
    updated, hidden_pre, active = update_forward(
        node_rows, message, moved_flat, w_node1, b_node, w_node2, row_mask
    )
    grad_out = jnp.where(
        row_mask, cotangent[0].reshape(-1, state_width), jnp.zeros((), jnp.bfloat16)
    )
    grad_rows, grad_message, grad_moved, grad_n1, grad_bn, grad_n2 = update_backward(
        node_rows, message, moved_flat, w_node1, w_node2, hidden_pre, active, grad_out
    )
    grad_moved_blocks = grad_moved.reshape(granules, block_rows, state_width)
    query_all, key_all = attend_back(local_nodes, keys_all, probs_all, low_all, grad_moved_blocks)
    slot_grad = (
        jnp.zeros((slot_count, block_rows, state_width), jnp.float32)
        .at[read_slot.reshape(-1)]
        .add(key_all.reshape(granules * GMAX, block_rows, state_width))
    )
    back_grad = lax.all_to_all(
        slot_grad.astype(jnp.bfloat16), "graph", split_axis=0, concat_axis=0, tiled=True
    ).astype(slot_grad.dtype)
    attention_grad = query_all + back_grad[send_slot]
    message_rows, grad_e1, grad_be, grad_e2 = message_backward(
        node_rows, w_edge1, w_edge2, sources, targets, gathered, summed, grad_message
    )
    total_grad = grad_rows + attention_grad.reshape(-1, state_width) + message_rows
    d_nodes = jnp.where(row_mask, total_grad, 0.0).astype(jnp.bfloat16)
    partial_grads = (grad_e1, grad_be, grad_e2, grad_n1, grad_bn, grad_n2)
    summed_all = lax.psum(
        (
            partial_grads[0],
            partial_grads[1],
            partial_grads[2],
            partial_grads[3],
            partial_grads[4],
            partial_grads[5],
        ),
        ("graph", "rep"),
    )
    replica_index = lax.axis_index("rep")
    replica_count = lax.axis_size("rep")
    shares = tuple(
        (
            lax.dynamic_slice_in_dim(
                summed_grad,
                replica_index * (summed_grad.shape[0] // replica_count),
                summed_grad.shape[0] // replica_count,
                0,
            )
            for summed_grad in summed_all
        )
    )
    scale_factor = (lax.axis_size("graph") * lax.axis_size("rep") * granules * block_rows) ** (-0.5)
    scaled = tuple((summed_grad * scale_factor for summed_grad in shares))
    return (
        updated.reshape(1, granules, block_rows, state_width),
        d_nodes.reshape(1, granules, block_rows, state_width),
        scaled[0],
        scaled[1],
        scaled[2],
        scaled[3],
        scaled[4],
        scaled[5],
    )


def solution(mesh):
    placed = (
        P("rep", "graph", None, None),
        P("rep", "graph", None, None),
        P("rep", "graph"),
        P("rep", "graph"),
        P("rep", "graph"),
        P("rep", "graph"),
        P("rep", "graph"),
        P(),
        P(),
        P(),
        P(),
        P(),
        P(),
    )
    return jax.shard_map(
        on_device,
        mesh=mesh,
        in_specs=placed,
        out_specs=(
            P("rep", "graph", None, None),
            P("rep", "graph", None, None),
            P("rep", None),
            P("rep"),
            P("rep", None),
            P("rep", None),
            P("rep"),
            P("rep", None),
        ),
        check_vma=False,
    )
```

profile of v0, /device:TPU:0, one launch (start us, length us, event | category | flops | bytes accessed | tf_op | source)
XLA Modules:
  0.0 223.0 jit_solution(15581898955150633358)
XLA Ops:
  10.2 5.2 %all-to-all-start = ((s32[8,4,1]{1,2,0:T(1,128)}), s32[8,4,1]{1,2,0:T(1,128)S(1)}, u32[]{:S(2)}, u32[]{:S(2)}) async-start(s32[8,4,1]{1,2,0:T(1,128)} %bitcast.11), calls=%async_computation | async-start | bytes 8192 | tf_op jit(solution)/shard_map/all_to_all | solution.py:183
  17.0 1.2 fusion.43
  18.2 1.2 convolution_convert_fusion.1
  20.5 1.2 gather_fusion.1
  21.6 1.2 gather_fusion
  22.8 2.4 %scatter_custom_fusion = f32[256,512]{1,0:T(8,128)S(1)} fusion(s32[256]{0:T(256)S(1)} %bitcast.123, bf16[256,512]{1,0:T(8,128)(2,1)S(1)} %gather_fusion.1, bf16[256,512]{1,0:T(8,128)(2,1)S(1)} %gather_fusion, f32[]{:T(128)} %constant.24.clone.1, f32[]{:T(128)} %constant.21.clone.1), kind=kCustom, calls=%fused_computation.59 | custom fusion | flops 1048576 | bytes 1048584 | tf_op jit(solution)/shard_map/scatter-add | solution.py:55
  27.3 2.1 scatter_fusion
  29.4 4.2 %all-to-all-start.1 = ((bf16[32,32,256]{2,1,0:T(8,128)(2,1)}), bf16[32,32,256]{2,1,0:T(8,128)(2,1)}, u32[]{:S(2)}, u32[]{:S(2)}) async-start(bf16[32,32,256]{2,1,0:T(8,128)(2,1)} %scatter_fusion), calls=%async_computation.1 | async-start | bytes 1048576 | tf_op jit(solution)/shard_map/all_to_all | solution.py:182
  36.2 7.2 %all-to-all-done.1 = bf16[32,32,256]{2,1,0:T(8,128)(2,1)} async-done(((bf16[32,32,256]{2,1,0:T(8,128)(2,1)}), bf16[32,32,256]{2,1,0:T(8,128)(2,1)}, u32[]{:S(2)}, u32[]{:S(2)}) %all-to-all-start.1) | async-done | bytes 524320 | tf_op jit(solution)/shard_map/all_to_all | solution.py:182
  43.4 1.6 gather_fusion.3
  49.2 1.7 fusion.52
  52.0 1.2 convolution_convert_fusion
  56.4 1.1 convolution_bitcast_fusion
  57.5 1.2 fusion.71
  58.7 1.2 gather_fusion.5
  59.8 2.6 %scatter_custom_fusion.4 = f32[256,512]{1,0:T(8,128)S(1)} fusion(s32[256]{0:T(256)} %bitcast.122, f32[]{:T(128)} %constant.21.clone.1, bf16[256,512]{1,0:T(8,128)(2,1)S(1)} %gather_fusion.5, bf16[256,512]{1,0:T(8,128)(2,1)S(1)} %gather_fusion.1, bf16[256,512]{1,0:T(8,128)(2,1)S(1)} %gather_fusion), kind=kCustom, calls=%fused_computation.68 | custom fusion | flops 1703936 | bytes 1311232 | tf_op jit(solution)/shard_map/scatter-add | solution.py:69
  62.4 2.8 %scatter_custom_fusion.5 = f32[256,512]{1,0:T(8,128)S(1)} fusion(s32[256]{0:T(256)} %bitcast.124, f32[]{:T(128)} %constant.21.clone.1, bf16[256,512]{1,0:T(8,128)(2,1)S(1)} %gather_fusion.5, bf16[256,512]{1,0:T(8,128)(2,1)S(1)} %gather_fusion.1, bf16[256,512]{1,0:T(8,128)(2,1)S(1)} %gather_fusion), kind=kCustom, calls=%fused_computation.66 | custom fusion | flops 1703936 | bytes 1311232 | tf_op jit(solution)/shard_map/scatter-add | solution.py:72
  67.0 1.3 pad_maximum_fusion
  68.4 2.3 %convolution_add_fusion = f32[8,64,256]{2,1,0:T(8,128)S(1)} fusion(f32[8,64,256]{2,1,0:T(8,128)S(1)} %fusion.52, f32[8,32,64]{2,1,0:T(8,128)} %fusion.74, bf16[1,8,32,256]{3,2,1,0:T(8,128)(2,1)S(1)} %copy-done.1, f32[8,32,64]{2,1,0:T(8,128)} %get-tuple-element.15, f32[8,32]{1,0:T(8,128)S(1)} %get-tuple-element.14), kind=kOutput, calls=%fused_computation.18 | convolution fusion | flops 8634687 | bytes 1311744 | tf_op jit(solution)/shard_map/gqk,gqh->gkh/dot_general | solution.py:40
  70.8 1.3 scatter_fusion.1
  73.1 3.6 %all-to-all-start.2 = ((bf16[32,32,256]{2,1,0:T(8,128)(2,1)}), bf16[32,32,256]{2,1,0:T(8,128)(2,1)S(1)}, u32[]{:S(2)}, u32[]{:S(2)}) async-start(bf16[32,32,256]{2,1,0:T(8,128)(2,1)} %convert_element_type.113), calls=%async_computation.2 | async-start | bytes 1048576 | tf_op jit(solution)/shard_map/all_to_all | solution.py:213
  76.7 46.2 %all-reduce = (f32[512]{0:T(512)S(1)}, f32[512]{0:T(512)S(1)}) all-reduce(f32[512]{0:T(512)S(1)} %convert_reduce_fusion.1, f32[512]{0:T(512)S(1)} %get-tuple-element.18), channel_id=1, replica_groups=mesh['graph'=8,'rep'=4] {'graph','rep'}, use_global_device_ids=true, to_apply=%region_11.12 | all-reduce | flops 1024 | bytes 8192 | tf_op jit(solution)/shard_map/psum | solution.py:223
  124.4 2.0 fusion.11
  126.4 1.1 convert_element_type.114
  127.6 1.8 gather_fusion.4
  129.4 2.2 fusion.6
  131.5 1.2 fusion.7
  133.7 75.8 %all-reduce.4.cloned.1.call-done = (f32[512,512]{1,0:T(8,128)}, f32[512,256]{1,0:T(8,128)}, f32[768,512]{1,0:T(8,128)}, f32[512,256]{1,0:T(8,128)}) async-done(((f32[512,512]{1,0:T(8,128)}, f32[512,256]{1,0:T(8,128)}, f32[768,512]{1,0:T(8,128)}, f32[512,256]{1,0:T(8,128)}), (f32[512,512]{1,0:T(8,128)}, f32[512,256]{1,0:T(8,128)}, f32[768,512]{1,0:T(8,128)}, ...) | async-done | bytes 3670032 | tf_op jit(solution)/shard_map/psum | solution.py:223
  209.5 1.7 dynamic-slice_multiply_fusion.1
  211.2 1.6 dynamic-slice_multiply_fusion.3
  212.8 1.6 dynamic-slice_multiply_fusion.2
  214.3 1.8 dynamic-slice_multiply_fusion
  (111 shorter events, 23.8 us)
Async XLA Ops:
  7.2 40.3 %copy-start = (bf16[512,256]{1,0:T(8,128)(2,1)S(1)}, bf16[512,256]{1,0:T(8,128)(2,1)}, u32[]{:S(2)}) copy-start(bf16[512,256]{1,0:T(8,128)(2,1)} %param.24) | copy-start | bytes 786436
  7.2 12.3 %copy-start.1 = (bf16[1,8,32,256]{3,2,1,0:T(8,128)(2,1)S(1)}, bf16[1,8,32,256]{3,2,1,0:T(8,128)(2,1)}, u32[]{:S(2)}) copy-start(bf16[1,8,32,256]{3,2,1,0:T(8,128)(2,1)} %param.13) | copy-start | bytes 393220
  7.2 12.3 %copy-start.6 = (bf16[512,512]{1,0:T(8,128)(2,1)S(1)}, bf16[512,512]{1,0:T(8,128)(2,1)}, u32[]{:S(2)}) copy-start(bf16[512,512]{1,0:T(8,128)(2,1)} %param.19) | copy-start | bytes 1572868
  7.2 12.2 %copy-start.24 = (s32[1,256]{1,0:T(1,128)S(1)}, s32[1,256]{1,0:T(1,128)}, u32[]{:S(2)}) copy-start(s32[1,256]{1,0:T(1,128)} %param.18) | copy-start | bytes 3076
  7.2 12.2 %copy-start.25 = (s32[1,256]{1,0:T(1,128)S(1)}, s32[1,256]{1,0:T(1,128)}, u32[]{:S(2)}) copy-start(s32[1,256]{1,0:T(1,128)} %param.17) | copy-start | bytes 3076
  7.2 12.3 %copy-start.20 = (f32[512]{0:T(512)S(1)}, f32[512]{0:T(512)}, u32[]{:S(2)}) copy-start(f32[512]{0:T(512)} %param.20) | copy-start | bytes 6148
  10.2 19.2 %all-to-all-start = ((s32[8,4,1]{1,2,0:T(1,128)}), s32[8,4,1]{1,2,0:T(1,128)S(1)}, u32[]{:S(2)}, u32[]{:S(2)}) async-start(s32[8,4,1]{1,2,0:T(1,128)} %bitcast.11), calls=%async_computation | async-start | bytes 8192 | tf_op jit(solution)/shard_map/all_to_all | solution.py:183
  21.6 3.6 %copy-start.9 = (bf16[512,256]{1,0:T(8,128)(2,1)S(1)}, bf16[512,256]{1,0:T(8,128)(2,1)}, u32[]{:S(2)}) copy-start(bf16[512,256]{1,0:T(8,128)(2,1)} %param.21) | copy-start | bytes 786436
  22.8 2.6 %copy-start.2 = (bf16[768,512]{1,0:T(8,128)(2,1)S(1)}, bf16[768,512]{1,0:T(8,128)(2,1)}, u32[]{:S(2)}) copy-start(bf16[768,512]{1,0:T(8,128)(2,1)} %param.22) | copy-start | bytes 2359300
  25.4 8.4 %copy-start.18 = (bf16[1,8,32,256]{3,2,1,0:T(8,128)(2,1)S(1)}, bf16[1,8,32,256]{3,2,1,0:T(8,128)(2,1)}, u32[]{:S(2)}) copy-start(bf16[1,8,32,256]{3,2,1,0:T(8,128)(2,1)} %param.14) | copy-start | bytes 393220
  29.4 14.0 %all-to-all-start.1 = ((bf16[32,32,256]{2,1,0:T(8,128)(2,1)}), bf16[32,32,256]{2,1,0:T(8,128)(2,1)}, u32[]{:S(2)}, u32[]{:S(2)}) async-start(bf16[32,32,256]{2,1,0:T(8,128)(2,1)} %scatter_fusion), calls=%async_computation.1 | async-start | bytes 1048576 | tf_op jit(solution)/shard_map/all_to_all | solution.py:182
  33.6 175.9 %all-reduce.4.cloned.1.call-start = ((), (), s32[]{:S(2)}) async-start(), calls=%async_computation.3 | async-start | bytes 7340032 | tf_op jit(solution)/shard_map/psum | solution.py:223
  33.7 2.2 copy-start.22
  34.0 13.5 %copy-start.11 = (bf16[256,256]{1,0:T(8,128)(2,1)}, bf16[256,256]{1,0:T(8,128)(2,1)S(1)}, u32[]{:S(2)}) copy-start(bf16[256,256]{1,0:T(8,128)(2,1)S(1)} %bitcast_select_fusion) | copy-start | bytes 393220
  35.9 11.3 %copy-start.8 = (f32[256,512]{1,0:T(8,128)S(1)}, f32[256,512]{1,0:T(8,128)}, u32[]{:S(2)}) copy-start(f32[256,512]{1,0:T(8,128)} %convolution_add_fusion.2) | copy-start | bytes 1572868
  35.9 11.3 %copy-start.21 = (f32[512]{0:T(512)S(1)}, f32[512]{0:T(512)}, u32[]{:S(2)}) copy-start(f32[512]{0:T(512)} %param.23) | copy-start | bytes 6148
  45.2 1.3 copy-start.10
  46.5 0.7 copy-start.16
  47.5 0.8 copy-start.14
  50.8 3.4 %copy-start.17 = (bf16[8,32,256]{2,1,0:T(8,128)(2,1)S(1)}, bf16[8,32,256]{2,1,0:T(8,128)(2,1)}, u32[]{:S(2)}) copy-start(bf16[8,32,256]{2,1,0:T(8,128)(2,1)} %copy-done.16) | copy-start | bytes 393220
  54.3 3.2 %copy-start.12 = (bf16[256,256]{1,0:T(8,128)(2,1)S(1)}, bf16[256,256]{1,0:T(8,128)(2,1)}, u32[]{:S(2)}) copy-start(bf16[256,256]{1,0:T(8,128)(2,1)} %copy-done.11) | copy-start | bytes 393220
  54.3 3.2 %copy-start.15 = (f32[256,512]{1,0:T(8,128)S(1)}, f32[256,512]{1,0:T(8,128)}, u32[]{:S(2)}) copy-start(f32[256,512]{1,0:T(8,128)} %copy-done.14) | copy-start | bytes 1572868
  65.4 1.4 copy-start.3
  65.4 1.3 copy-start.4
  65.4 1.6 copy-start.5
  68.3 2.5 %copy-start.26 = (s32[16]{0:T(128)S(1)}, s32[16]{0:T(128)}, u32[]{:S(2)}) copy-start(s32[16]{0:T(128)} %fusion.60) | copy-start | bytes 196
  73.1 51.1 %copy-start.7 = (bf16[512,512]{1,0:T(8,128)(2,1)S(1)}, bf16[512,512]{1,0:T(8,128)(2,1)}, u32[]{:S(2)}) copy-start(bf16[512,512]{1,0:T(8,128)(2,1)} %param.19) | copy-start | bytes 1572868
  73.1 51.3 %copy-start.23 = (pred[256]{0:T(512)(128)(4,1)S(1)}, pred[256]{0:T(512)(128)(4,1)}, u32[]{:S(2)}) copy-start(pred[256]{0:T(512)(128)(4,1)} %copy-done.22) | copy-start | bytes 772
  73.1 53.4 %all-to-all-start.2 = ((bf16[32,32,256]{2,1,0:T(8,128)(2,1)}), bf16[32,32,256]{2,1,0:T(8,128)(2,1)S(1)}, u32[]{:S(2)}, u32[]{:S(2)}) async-start(bf16[32,32,256]{2,1,0:T(8,128)(2,1)} %convert_element_type.113), calls=%async_computation.2 | async-start | bytes 1048576 | tf_op jit(solution)/shard_map/all_to_all | solution.py:213
  126.4 2.9 %copy-start.19 = (bf16[256,256]{1,0:T(8,128)(2,1)S(1)}, bf16[256,256]{1,0:T(8,128)(2,1)}, u32[]{:S(2)}) copy-start(bf16[256,256]{1,0:T(8,128)(2,1)} %get-tuple-element.17) | copy-start | bytes 393220
  126.4 5.1 %copy-start.13 = (bf16[256,256]{1,0:T(8,128)(2,1)S(1)}, bf16[256,256]{1,0:T(8,128)(2,1)}, u32[]{:S(2)}) copy-start(bf16[256,256]{1,0:T(8,128)(2,1)} %copy-done.11) | copy-start | bytes 393220
Sparse Core Ops, SparseCore 0:
  68.5 141.0 all-reduce.3
where the time goes:
time: 224 us; the launch traced here: 223 us
  waiting for transfers between devices  83.1 us (37%)
  blocking collectives  46.2 us (21%)
  other arithmetic  26.5 us (12%)
  matrix products  25 us (11%)
  local copies, waits for them, and re-layouts  14.6 us (7%)
  between operations  14.6 us (7%)
  starting transfers between devices  13 us (6%)
    psum x1, waiting for transfers between devices, on_device(): lax.psum((partial_grads[0], partial_grads[1], partial_grads[2], partial_g...  75.8 us
    psum x1, blocking collectives, on_device(): lax.psum((partial_grads[0], partial_grads[1], partial_grads[2], partial_g...  46.2 us
    mul x6, other arithmetic, on_device(): scaled = tuple((summed_grad * scale_factor for summed_grad in shares))  7.76 us
    all_to_all x1, waiting for transfers between devices, on_device(): lax.all_to_all(outgoing, 'graph', split_axis=0, concat_axis=0, tiled=True)  7.23 us
    all_to_all x1, starting transfers between devices, on_device(): lax.all_to_all(lives_out, 'graph', split_axis=0, concat_axis=0, tiled=True)  5.2 us
  transfers between devices with their start and end apart: 4, of which 2 were waited for; matrix products, arithmetic and copies ran while one was open for 14% of the time, Pallas kernels for 0%

commit v1 on v0

--- a/solution.py
+++ b/solution.py
@@ -221,15 +221,18 @@
     d_nodes = jnp.where(row_mask, total_grad, 0.0).astype(jnp.bfloat16)
     partial_grads = (grad_e1, grad_be, grad_e2, grad_n1, grad_bn, grad_n2)
     summed_all = lax.psum(
-        (
-            partial_grads[0],
-            partial_grads[1],
-            partial_grads[2],
-            partial_grads[3],
-            partial_grads[4],
-            partial_grads[5],
+        lax.psum(
+            (
+                partial_grads[0],
+                partial_grads[1],
+                partial_grads[2],
+                partial_grads[3],
+                partial_grads[4],
+                partial_grads[5],
+            ),
+            "rep",
         ),
-        ("graph", "rep"),
+        "graph",
     )
     replica_index = lax.axis_index("rep")
     replica_count = lax.axis_size("rep")

time: 224 us -> 298 us (1.33)
  waiting for transfers between devices: 83.1 us -> 182 us
  blocking collectives: 46.2 us -> 22.8 us
    psum x1, waiting for transfers between devices: 75.8 us -> 134 us  [on_device(): lax.psum((partial_grads[0], partial_grads[1], partial_grads[2], partial_g...]
    psum x0 -> x1, waiting for transfers between devices: none -> 41.2 us  [on_device(): lax.psum(lax.psum((partial_grads[0], partial_grads[1], partial_grads[2],...]
    psum x1, blocking collectives: 46.2 us -> 9.67 us  [on_device(): lax.psum((partial_grads[0], partial_grads[1], partial_grads[2], partial_g...]
    psum x0 -> x1, blocking collectives: none -> 13.1 us  [on_device(): lax.psum(lax.psum((partial_grads[0], partial_grads[1], partial_grads[2],...]
  transfers between devices with their start and end apart: 4 -> 5, of which waited for: 2 -> 3; matrix products, arithmetic and copies ran while one was open for 14% -> 12% of each run, Pallas kernels for 0% -> 0%
where the time goes in v1:
time: 298 us; the launch traced here: 297 us
  waiting for transfers between devices  182 us (61%)
  other arithmetic  27 us (9%)
  matrix products  23.3 us (8%)
  blocking collectives  22.8 us (8%)
  between operations  14.6 us (5%)
  local copies, waits for them, and re-layouts  14.4 us (5%)
  starting transfers between devices  13.3 us (4%)
    psum x1, waiting for transfers between devices, on_device(): lax.psum((partial_grads[0], partial_grads[1], partial_grads[2], partial_g...  134 us
    psum x1, waiting for transfers between devices, on_device(): lax.psum(lax.psum((partial_grads[0], partial_grads[1], partial_grads[2],...  41.2 us
    psum x1, blocking collectives, on_device(): lax.psum(lax.psum((partial_grads[0], partial_grads[1], partial_grads[2],...  13.1 us
    psum x1, blocking collectives, on_device(): lax.psum((partial_grads[0], partial_grads[1], partial_grads[2], partial_g...  9.67 us
    mul x6, other arithmetic, on_device(): scaled = tuple((summed_grad * scale_factor for summed_grad in shares))  7.77 us
    all_to_all x1, waiting for transfers between devices, on_device(): lax.all_to_all(outgoing, 'graph', split_axis=0, concat_axis=0, tiled=True)  6.64 us
  transfers between devices with their start and end apart: 5, of which 3 were waited for; matrix products, arithmetic and copies ran while one was open for 12% of the time, Pallas kernels for 0%

profile of v1, /device:TPU:0, one launch (start us, length us, event | category | flops | bytes accessed | tf_op | source)
XLA Modules:
  0.0 297.2 jit_solution(1531489678884279180)
XLA Ops:
  10.2 5.2 %all-to-all-start = ((s32[8,4,1]{1,2,0:T(1,128)}), s32[8,4,1]{1,2,0:T(1,128)S(1)}, u32[]{:S(2)}, u32[]{:S(2)}) async-start(s32[8,4,1]{1,2,0:T(1,128)} %bitcast.11), calls=%async_computation | async-start | bytes 8192 | tf_op jit(solution)/shard_map/all_to_all | solution.py:183
  15.4 1.3 iota_compare_fusion
  17.4 1.2 fusion.43
  18.6 1.2 convolution_convert_fusion.1
  20.3 1.2 gather_fusion.1
  21.5 1.2 gather_fusion
  22.7 2.4 scatter_custom_fusion
  26.4 2.1 scatter_fusion
  28.5 4.2 %all-to-all-start.1 = ((bf16[32,32,256]{2,1,0:T(8,128)(2,1)}), bf16[32,32,256]{2,1,0:T(8,128)(2,1)}, u32[]{:S(2)}, u32[]{:S(2)}) async-start(bf16[32,32,256]{2,1,0:T(8,128)(2,1)} %scatter_fusion), calls=%async_computation.1 | async-start | bytes 1048576 | tf_op jit(solution)/shard_map/all_to_all | solution.py:182
  35.9 6.6 %all-to-all-done.1 = bf16[32,32,256]{2,1,0:T(8,128)(2,1)} async-done(((bf16[32,32,256]{2,1,0:T(8,128)(2,1)}), bf16[32,32,256]{2,1,0:T(8,128)(2,1)}, u32[]{:S(2)}, u32[]{:S(2)}) %all-to-all-start.1) | async-done | bytes 524320 | tf_op jit(solution)/shard_map/all_to_all | solution.py:182
  42.6 1.6 gather_fusion.3
  46.6 2.0 convert_reduce_fusion
  53.8 1.2 gather_fusion.5
  55.0 2.6 scatter_custom_fusion.4
  57.6 2.6 scatter_custom_fusion.5
  61.8 1.3 pad_maximum_fusion
  63.9 1.9 fusion.73
  66.7 134.0 %all-reduce.9.cloned.1.call-done = (f32[512,512]{1,0:T(8,128)}, f32[512,256]{1,0:T(8,128)}, f32[768,512]{1,0:T(8,128)}, f32[512,256]{1,0:T(8,128)}) async-done(((f32[512,512]{1,0:T(8,128)}, f32[512,256]{1,0:T(8,128)}, f32[768,512]{1,0:T(8,128)}, f32[512,256]{1,0:T(8,128)}), (f32[512,512]{1,0:T(8,128)}, f32[512,256]{1,0:T(8,128)}, f32[768,512]{1,0:T(8,128)}, ...) | async-done | bytes 3670032 | tf_op jit(solution)/shard_map/psum | solution.py:224
  200.7 2.2 convolution_add_fusion
  203.0 1.3 scatter_fusion.1
  205.3 3.7 %all-to-all-start.2 = ((bf16[32,32,256]{2,1,0:T(8,128)(2,1)}), bf16[32,32,256]{2,1,0:T(8,128)(2,1)S(1)}, u32[]{:S(2)}, u32[]{:S(2)}) async-start(bf16[32,32,256]{2,1,0:T(8,128)(2,1)} %convert_element_type.113), calls=%async_computation.2 | async-start | bytes 1048576 | tf_op jit(solution)/shard_map/all_to_all | solution.py:213
  209.0 9.7 %all-reduce.2 = (f32[512]{0:T(512)S(1)}, f32[512]{0:T(512)S(1)}) all-reduce(f32[512]{0:T(512)S(1)} %convert_reduce_fusion.1, f32[512]{0:T(512)S(1)} %copy-done.21), channel_id=1, replica_groups=mesh['graph'=8,'rep'=4] {'rep'}, use_global_device_ids=true, to_apply=%region_12.13 | all-reduce | flops 1024 | bytes 8192 | tf_op jit(solution)/shard_map/psum | solution.py:224
  218.7 13.1 %all-reduce = (f32[512]{0:T(512)S(1)}, f32[512]{0:T(512)S(1)}) all-reduce(f32[512]{0:T(512)S(1)} %get-tuple-element.14, f32[512]{0:T(512)S(1)} %get-tuple-element.15), channel_id=1, replica_groups=mesh['graph'=8,'rep'=4] {'graph'}, use_global_device_ids=true, to_apply=%region_13.14 | all-reduce | flops 1024 | bytes 8192 | tf_op jit(solution)/shard_map/psum | solution.py:223
  233.2 2.0 fusion.11
  236.4 1.9 gather_fusion.4
  238.3 2.2 fusion.6
  240.5 1.2 fusion.7
  242.6 41.2 %all-reduce.7.cloned.1.call-done = (f32[512,512]{1,0:T(8,128)}, f32[512,256]{1,0:T(8,128)}, f32[768,512]{1,0:T(8,128)}, f32[512,256]{1,0:T(8,128)}) async-done(((f32[512,512]{1,0:T(8,128)}, f32[512,256]{1,0:T(8,128)}, f32[768,512]{1,0:T(8,128)}, f32[512,256]{1,0:T(8,128)}), (f32[512,512]{1,0:T(8,128)}, f32[512,256]{1,0:T(8,128)}, f32[768,512]{1,0:T(8,128)}, ...) | async-done | bytes 3670032 | tf_op jit(solution)/shard_map/psum | solution.py:223
  283.8 1.7 dynamic-slice_multiply_fusion.1
  285.5 1.6 dynamic-slice_multiply_fusion.3
  287.0 1.6 dynamic-slice_multiply_fusion.2
  288.6 1.8 dynamic-slice_multiply_fusion
  (111 shorter events, 23.9 us)
Async XLA Ops:
  7.2 39.4 %copy-start = (bf16[512,256]{1,0:T(8,128)(2,1)S(1)}, bf16[512,256]{1,0:T(8,128)(2,1)}, u32[]{:S(2)}) copy-start(bf16[512,256]{1,0:T(8,128)(2,1)} %param.24) | copy-start | bytes 786436
  7.2 12.7 %copy-start.1 = (bf16[1,8,32,256]{3,2,1,0:T(8,128)(2,1)S(1)}, bf16[1,8,32,256]{3,2,1,0:T(8,128)(2,1)}, u32[]{:S(2)}) copy-start(bf16[1,8,32,256]{3,2,1,0:T(8,128)(2,1)} %param.13) | copy-start | bytes 393220
  7.2 12.7 %copy-start.5 = (bf16[512,512]{1,0:T(8,128)(2,1)S(1)}, bf16[512,512]{1,0:T(8,128)(2,1)}, u32[]{:S(2)}) copy-start(bf16[512,512]{1,0:T(8,128)(2,1)} %param.19) | copy-start | bytes 1572868
  7.2 12.7 %copy-start.22 = (s32[1,256]{1,0:T(1,128)S(1)}, s32[1,256]{1,0:T(1,128)}, u32[]{:S(2)}) copy-start(s32[1,256]{1,0:T(1,128)} %param.18) | copy-start | bytes 3076
  7.2 12.7 %copy-start.23 = (s32[1,256]{1,0:T(1,128)S(1)}, s32[1,256]{1,0:T(1,128)}, u32[]{:S(2)}) copy-start(s32[1,256]{1,0:T(1,128)} %param.17) | copy-start | bytes 3076
  7.2 12.7 %copy-start.17 = (f32[512]{0:T(512)S(1)}, f32[512]{0:T(512)}, u32[]{:S(2)}) copy-start(f32[512]{0:T(512)} %param.20) | copy-start | bytes 6148
  10.2 18.3 %all-to-all-start = ((s32[8,4,1]{1,2,0:T(1,128)}), s32[8,4,1]{1,2,0:T(1,128)S(1)}, u32[]{:S(2)}, u32[]{:S(2)}) async-start(s32[8,4,1]{1,2,0:T(1,128)} %bitcast.11), calls=%async_computation | async-start | bytes 8192 | tf_op jit(solution)/shard_map/all_to_all | solution.py:183
  17.4 2.9 copy-start.19
  21.5 3.6 %copy-start.7 = (bf16[512,256]{1,0:T(8,128)(2,1)S(1)}, bf16[512,256]{1,0:T(8,128)(2,1)}, u32[]{:S(2)}) copy-start(bf16[512,256]{1,0:T(8,128)(2,1)} %param.21) | copy-start | bytes 786436
  22.7 2.6 copy-start.2
  25.3 7.7 %copy-start.15 = (bf16[1,8,32,256]{3,2,1,0:T(8,128)(2,1)S(1)}, bf16[1,8,32,256]{3,2,1,0:T(8,128)(2,1)}, u32[]{:S(2)}) copy-start(bf16[1,8,32,256]{3,2,1,0:T(8,128)(2,1)} %param.14) | copy-start | bytes 393220
  25.6 7.2 %copy-start.24 = (pred[8,32]{1,0:T(8,128)(4,1)S(1)}, pred[8,32]{1,0:T(8,128)(4,1)}, u32[]{:S(2)}) copy-start(pred[8,32]{1,0:T(8,128)(4,1)} %iota_compare_fusion) | copy-start | bytes 772
  28.5 14.0 %all-to-all-start.1 = ((bf16[32,32,256]{2,1,0:T(8,128)(2,1)}), bf16[32,32,256]{2,1,0:T(8,128)(2,1)}, u32[]{:S(2)}, u32[]{:S(2)}) async-start(bf16[32,32,256]{2,1,0:T(8,128)(2,1)} %scatter_fusion), calls=%async_computation.1 | async-start | bytes 1048576 | tf_op jit(solution)/shard_map/all_to_all | solution.py:182
  32.7 167.9 %all-reduce.9.cloned.1.call-start = ((), (), s32[]{:S(2)}) async-start(), calls=%async_computation.4 | async-start | bytes 7340032 | tf_op jit(solution)/shard_map/psum | solution.py:224
  35.7 10.7 %copy-start.18 = (f32[512]{0:T(512)S(1)}, f32[512]{0:T(512)}, u32[]{:S(2)}) copy-start(f32[512]{0:T(512)} %param.23) | copy-start | bytes 6148
  45.7 0.7 copy-start.12
  46.6 6.1 %copy-start.11 = (f32[256,512]{1,0:T(8,128)}, f32[256,512]{1,0:T(8,128)S(1)}, u32[]{:S(2)}) copy-start(f32[256,512]{1,0:T(8,128)S(1)} %fusion.2) | copy-start | bytes 1572868
  46.6 2.3 copy-start.8
  48.6 1.6 copy-start.13
  50.3 2.4 copy-start.9
  60.4 1.3 copy-start.3
  60.4 1.3 copy-start.4
  63.1 0.7 copy-start.20
  63.1 220.7 %all-reduce.7.cloned.1.call-start = ((), (), s32[]{:S(2)}) async-start(), calls=%async_computation.3 | async-start | bytes 7340032 | tf_op jit(solution)/shard_map/psum | solution.py:223
  66.0 134.7 %copy-start.14 = (f32[8,32,64]{2,1,0:T(8,128)}, f32[8,32,64]{2,1,0:T(8,128)S(1)}, u32[]{:S(2)}) copy-start(f32[8,32,64]{2,1,0:T(8,128)S(1)} %fusion.74) | copy-start | bytes 196612
  204.4 4.6 %copy-start.21 = (f32[512]{0:T(512)S(1)}, f32[512]{0:T(512)}, u32[]{:S(2)}) copy-start(f32[512]{0:T(512)} %get-tuple-element.24) | copy-start | bytes 6148
  204.4 28.6 %copy-start.6 = (bf16[512,512]{1,0:T(8,128)(2,1)S(1)}, bf16[512,512]{1,0:T(8,128)(2,1)}, u32[]{:S(2)}) copy-start(bf16[512,512]{1,0:T(8,128)(2,1)} %param.19) | copy-start | bytes 1572868
  205.3 30.0 %all-to-all-start.2 = ((bf16[32,32,256]{2,1,0:T(8,128)(2,1)}), bf16[32,32,256]{2,1,0:T(8,128)(2,1)S(1)}, u32[]{:S(2)}, u32[]{:S(2)}) async-start(bf16[32,32,256]{2,1,0:T(8,128)(2,1)} %convert_element_type.113), calls=%async_computation.2 | async-start | bytes 1048576 | tf_op jit(solution)/shard_map/all_to_all | solution.py:213
  235.2 3.1 %copy-start.16 = (bf16[256,256]{1,0:T(8,128)(2,1)S(1)}, bf16[256,256]{1,0:T(8,128)(2,1)}, u32[]{:S(2)}) copy-start(bf16[256,256]{1,0:T(8,128)(2,1)} %get-tuple-element.23) | copy-start | bytes 393220
  235.2 5.3 %copy-start.10 = (bf16[256,256]{1,0:T(8,128)(2,1)S(1)}, bf16[256,256]{1,0:T(8,128)(2,1)}, u32[]{:S(2)}) copy-start(bf16[256,256]{1,0:T(8,128)(2,1)} %bitcast_select_fusion) | copy-start | bytes 393220
Sparse Core Ops, SparseCore 0:
  63.2 137.3 all-reduce.8
  204.3 79.4 all-reduce.6
